TPU v7x, 32 devices: a whole 2x2x4 slice. The times are simulated.
32 devices in a mesh: row: 4 (over y, x), col: 4 (over z), grp: 2 (over core).
Axes of the slice: x: 2, y: 2, z: 4, core: 2. Of those that a mesh axis runs over, the one named last changes fastest.
Arguments:
- krylov_basis: float32 [30, 8, 8192], P(None, None, 'row'), may hold values from -6 to 6
- lattice: int32 [3, 8192], P(None, 'row'), may hold values from 0 to 95, as said below
- strength_index: int32 [8192], P('row'), may hold values from 0 to 15
- strength_table: float32 [16], replicated, may hold values from 0.05 to 0.4
Outputs:
- new_block: float32 [8, 8192], P(None, 'row')
- hessenberg: float32 [30, 2, 4, 4], replicated
- block_gram: float32 [2, 4, 4], replicated
Inputs may be any that keep to these rules, and one draw needn't show every extreme that they name: The 8192 scatterers stand on distinct lattice points.
All inputs are finite; a program needn't handle non-finite values.
Results may differ from a plain program's by a relative error of at most 0.0003.
Values may be sent and summed in bfloat16 or wider, within the bound.
A program may use at most 64 MiB of HBM per device.

v0:
```python
import math

import jax
import jax.numpy as jnp
from jax import lax
from jax.sharding import PartitionSpec as P

wave_number = 2.0
highest = lax.Precision.HIGHEST


def strength_of(strength_table, strength_index):
    matches = (
        strength_index[:, None] == jnp.arange(strength_table.shape[0], dtype=jnp.int32)[None, :]
    )
    return jnp.sum(
        jnp.where(matches, strength_table[None, :], jnp.zeros((), strength_table.dtype)), axis=1
    )


def green_pair(target, source):
    squared = jnp.zeros((target.shape[1], source.shape[1]), jnp.float32)
    for axis_id in range(3):
        offset = target[axis_id][:, None] - source[axis_id][None, :]
        squared = squared + offset * offset
    distance = jnp.sqrt(jnp.maximum(squared, 1.0))
    phases = wave_number * distance
    inverse = 1.0 / distance
    distinct = squared > 0.5
    real_part = jnp.where(distinct, jnp.cos(phases) * inverse, 0.0)
    imag_part = jnp.where(distinct, jnp.sin(phases) * inverse, 0.0)
    return jnp.concatenate([real_part, imag_part], 0).astype(jnp.bfloat16)


def combine(product, tile_size):
    half_rows = product.shape[0] // 2
    direct = product[:, :tile_size]
    turned = product[:, tile_size:]
    return jnp.concatenate(
        [direct[:half_rows] - turned[half_rows:], direct[half_rows:] + turned[:half_rows]], 0
    )


def scatter_block(target, source, weighted):
    stacked = green_pair(target, source)
    product = lax.dot_general(
        weighted, stacked, (((1,), (1,)), ((), ())), preferred_element_type=jnp.float32
    )
    return combine(product, target.shape[1])


def project(krylov_basis, field):
    return jnp.einsum("jan,bn->jab", krylov_basis, field, precision=highest)


def self_gram(field):
    return jnp.dot(field, field.T, precision=highest)


def complex_parts(gram):
    half_rows = gram.shape[-1] // 2
    real_part = gram[..., :half_rows, :half_rows] + gram[..., half_rows:, half_rows:]
    imag_part = gram[..., :half_rows, half_rows:] - gram[..., half_rows:, :half_rows]
    return (real_part, imag_part)


def subtract(krylov_basis, field, real_part, imag_part):
    upper = jnp.concatenate([real_part, imag_part], -1)
    lower = jnp.concatenate([-imag_part, real_part], -1)
    mixing = jnp.concatenate([upper, lower], -2)
    return field - jnp.einsum("jab,jan->bn", mixing, krylov_basis, precision=highest)


def row_first_sum(value):
    return lax.psum(value, "row")


def row_second_sum(value):
    return lax.psum(value, "row")


def row_norm_sum(value):
    return lax.psum(value, "row")


def orthogonalize(krylov_basis, initial, point_total, summers):
    sum_first, sum_second, sum_norm = summers
    once_real, once_imag = complex_parts(sum_first(project(krylov_basis, initial)) / point_total)
    once = subtract(krylov_basis, initial, once_real, once_imag)
    twice_real, twice_imag = complex_parts(sum_second(project(krylov_basis, once)) / point_total)
    new_block = subtract(krylov_basis, once, twice_real, twice_imag)
    norm_real, norm_imag = complex_parts(sum_norm(self_gram(new_block)) / point_total)
    hessenberg = jnp.stack([once_real + twice_real, once_imag + twice_imag], 1)
    block_gram = jnp.stack([norm_real, norm_imag], 0)
    return (new_block, hessenberg, block_gram)


def local(krylov_basis, lattice, strength_index, strength_table):
    local_rows = krylov_basis.shape[2]
    column_parts = lax.axis_size(("col", "grp"))
    block_size = local_rows // column_parts
    column_id = lax.axis_index(("col", "grp"))
    point_total = local_rows * lax.axis_size("row")
    direction = krylov_basis[krylov_basis.shape[0] - 1]
    channel_rows = direction.shape[0]
    weighted = (direction * strength_of(strength_table, strength_index)[None, :]).astype(
        jnp.bfloat16
    )
    slice_start = column_id * block_size
    own_weights = lax.dynamic_slice_in_dim(weighted, slice_start, block_size, 1)
    own_sites = lax.dynamic_slice_in_dim(lattice, slice_start, block_size, 1).astype(jnp.bfloat16)
    packed = jnp.concatenate([own_weights, own_sites], 0)
    located = lattice.astype(jnp.float32)
    tile_size = math.gcd(local_rows, 512)
    targets = located.reshape(3, local_rows // tile_size, tile_size).transpose(1, 0, 2)
    portion = lax.all_gather(packed, "row", axis=1, tiled=True)
    source_weights = portion[:channel_rows]
    source_sites = portion[channel_rows:].astype(jnp.float32)
    tiles = lax.map(lambda target: scatter_block(target, source_sites, source_weights), targets)
    scattered = tiles.transpose(1, 0, 2).reshape(channel_rows, local_rows)
    initial = direction - lax.psum(scattered, ("col", "grp"))
    summers = (row_first_sum, row_second_sum, row_norm_sum)
    new_block, hessenberg, block_gram = orthogonalize(krylov_basis, initial, point_total, summers)
    return (new_block, hessenberg, block_gram)


def solution(mesh):
    in_specs = (P(None, None, "row"), P(None, "row"), P("row"), P())
    out_specs = (P(None, "row"), P(), P())
    return jax.shard_map(local, mesh=mesh, in_specs=in_specs, out_specs=out_specs, check_vma=False)
```

profile of v0, /device:TPU:0, one launch (start us, length us, event | category | flops | bytes accessed | tf_op | source)
XLA Modules:
  0.0 180.9 jit_solution(17588530397306674130)
XLA Ops:
  7.2 0.0 all-reduce.2.cloned.1.call-start
  7.2 0.8 slice_bitcast_fusion
  8.1 0.8 select_reduce_fusion
  8.9 0.1 dynamic-slice.3
  9.0 0.7 dynamic-slice_convert_fusion
  9.7 9.7 %all_gather.3 = bf16[11,1024]{1,0:T(8,128)(2,1)S(1)} all-gather(bf16[11,256]{1,0:T(8,128)(2,1)S(1)} %pad_maximum_fusion.1), channel_id=1, replica_groups=mesh['row'=4,'col'=4,'grp'=2] {'row'}, dimensions={1}, use_global_device_ids=true | all-gather | bytes 28160 | tf_op jit(solution)/shard_map/all_gather | solution.py:116
  19.4 0.8 convert_element_type.13
  20.2 0.0 copy-start
  20.2 41.6 %while.10 = (s32[]{:T(128)}, f32[4,8,512]{2,1,0:T(8,128)S(1)}, f32[4,3,512]{2,1,0:T(4,128)S(1)}, f32[3,1024]{1,0:T(4,128)S(1)}, bf16[8,1024]{1,0:T(8,128)(2,1)S(1)}, /*index=5*/s32[]{:T(128)}, s32[]{:T(128)}, s32[]{}, s32[]{}) while((s32[]{:T(128)}, f32[4,8,512]{2,1,0:T(8,128)S(1)}, f32[4,3,512]{2,1,0:T(4,128)S(1)}, f32[3,1024]{1,0:T(4,128)S(1)}, ...), condition=%wide.region_2.3_spmd, body=%wide.region_1.2_spmd.sunk | while | flops 30416900 | bytes 4380805 | solution.py:119
  20.2 9.7 %select_convert_fusion.3 = (bf16[512,1024]{1,0:T(8,128)(2,1)S(1)}, bf16[512,1024]{1,0:T(8,128)(2,1)S(1)}) fusion(f32[1024]{0:T(1024)S(1)} %bitcast.76, f32[512]{0:T(512)S(1)} %bitcast.81, f32[1024]{0:T(1024)S(1)} %bitcast.77, f32[512]{0:T(512)S(1)} %bitcast.80, f32[1024]{0:T(1024)S(1)} %bitcast.75, f32[512]{0:T(512)S(1)} %bitcast.79), kind=kLoop, calls=%fused_computation.5.clone.1 | loop fusion | flops 9437184 | bytes 2115584 | tf_op jit(solution)/shard_map/convert
  29.9 0.6 fusion.60
  30.6 9.7 %select_convert_fusion.3 = (bf16[512,1024]{1,0:T(8,128)(2,1)S(1)}, bf16[512,1024]{1,0:T(8,128)(2,1)S(1)}) fusion(f32[1024]{0:T(1024)S(1)} %bitcast.76, f32[512]{0:T(512)S(1)} %bitcast.81, f32[1024]{0:T(1024)S(1)} %bitcast.77, f32[512]{0:T(512)S(1)} %bitcast.80, f32[1024]{0:T(1024)S(1)} %bitcast.75, f32[512]{0:T(512)S(1)} %bitcast.79), kind=kLoop, calls=%fused_computation.5.clone.1 | loop fusion | flops 9437184 | bytes 2115584 | tf_op jit(solution)/shard_map/convert
  40.3 0.6 fusion.60
  41.0 9.7 %select_convert_fusion.3 = (bf16[512,1024]{1,0:T(8,128)(2,1)S(1)}, bf16[512,1024]{1,0:T(8,128)(2,1)S(1)}) fusion(f32[1024]{0:T(1024)S(1)} %bitcast.76, f32[512]{0:T(512)S(1)} %bitcast.81, f32[1024]{0:T(1024)S(1)} %bitcast.77, f32[512]{0:T(512)S(1)} %bitcast.80, f32[1024]{0:T(1024)S(1)} %bitcast.75, f32[512]{0:T(512)S(1)} %bitcast.79), kind=kLoop, calls=%fused_computation.5.clone.1 | loop fusion | flops 9437184 | bytes 2115584 | tf_op jit(solution)/shard_map/convert
  50.7 0.6 fusion.60
  51.4 9.7 %select_convert_fusion.3 = (bf16[512,1024]{1,0:T(8,128)(2,1)S(1)}, bf16[512,1024]{1,0:T(8,128)(2,1)S(1)}) fusion(f32[1024]{0:T(1024)S(1)} %bitcast.76, f32[512]{0:T(512)S(1)} %bitcast.81, f32[1024]{0:T(1024)S(1)} %bitcast.77, f32[512]{0:T(512)S(1)} %bitcast.80, f32[1024]{0:T(1024)S(1)} %bitcast.75, f32[512]{0:T(512)S(1)} %bitcast.79), kind=kLoop, calls=%fused_computation.5.clone.1 | loop fusion | flops 9437184 | bytes 2115584 | tf_op jit(solution)/shard_map/convert
  61.1 0.6 fusion.60
  61.8 0.0 copy-start.3
  61.8 0.6 copy-done.3
  62.4 0.0 all-reduce.2.cloned.1.call-update
  62.4 55.1 %all-reduce.2.cloned.1.call-done = f32[8,2048]{1,0:T(8,128)} async-done(((f32[8,2048]{1,0:T(8,128)}), f32[8,2048]{1,0:T(8,128)}) %all-reduce.2.cloned.1.call-update) | async-done | bytes 65552 | tf_op jit(solution)/shard_map/psum | solution.py:121
  117.6 0.0 copy-done
  117.6 0.0 copy-start.2
  117.6 5.7 %fusion.19 = f32[30,8,8]{0,2,1:T(8,128)S(1)} fusion(f32[30,8,2048]{2,1,0:T(8,128)S(1)} %copy-done, f32[8,2048]{1,0:T(8,128)} %all-reduce.2.cloned.1.call-done), kind=kOutput, calls=%fused_computation.29 | convolution fusion | flops 47202304 | bytes 2104832 | tf_op jit(solution)/shard_map/jan,bn->jab/dot_general | solution.py:53
  123.3 16.2 %psum.29 = f32[30,8,8]{0,2,1:T(8,128)S(1)} all-reduce(f32[30,8,8]{0,2,1:T(8,128)S(1)} %fusion.19), channel_id=1, replica_groups=mesh['row'=4,'col'=4,'grp'=2] {'row'}, use_global_device_ids=true, to_apply=%region_4.5 | all-reduce | flops 1920 | bytes 15360 | tf_op jit(solution)/shard_map/psum | solution.py:75
  139.5 0.0 copy-done.2
  139.6 2.5 %fusion.12 = f32[8,2048]{1,0:T(8,128)S(1)} fusion(f32[30,8,2048]{2,1,0:T(8,128)S(1)} %copy-done, f32[30,4,4]{0,2,1:T(4,128)S(1)} %get-tuple-element.59, f32[30,4,4]{0,2,1:T(4,128)S(1)} %get-tuple-element.45, f32[30,4,4]{0,2,1:T(4,128)S(1)} %get-tuple-element.46, f32[8,2048]{1,0:T(8,128)S(1)} %copy-done.2), kind=kOutput, calls=%fused_computation.22 | convolution fusion | flops 47224448 | bytes 2187264 | tf_op jit(solution)/shard_map/jab,jan->bn/dot_general | solution.py:71
  142.0 4.8 %fusion.22 = f32[30,8,8]{0,2,1:T(8,128)S(1)} fusion(f32[30,8,2048]{2,1,0:T(8,128)S(1)} %copy-done, f32[8,2048]{1,0:T(8,128)S(1)} %fusion.12), kind=kOutput, calls=%fused_computation.30 | convolution fusion | flops 47185920 | bytes 2039296 | tf_op jit(solution)/shard_map/jan,bn->jab/dot_general | solution.py:53
  146.8 14.3 %psum.30 = f32[30,8,8]{0,2,1:T(8,128)S(1)} all-reduce(f32[30,8,8]{0,2,1:T(8,128)S(1)} %fusion.22), channel_id=1, replica_groups=mesh['row'=4,'col'=4,'grp'=2] {'row'}, use_global_device_ids=true, to_apply=%region_5.6 | all-reduce | flops 1920 | bytes 15360 | tf_op jit(solution)/shard_map/psum | solution.py:79
  161.1 2.5 %fusion.11 = f32[8,2048]{1,0:T(8,128)S(1)} fusion(f32[8,2048]{1,0:T(8,128)S(1)} %fusion.12, f32[30,8,2048]{2,1,0:T(8,128)S(1)} %copy-done, f32[30,4,4]{0,2,1:T(4,128)S(1)} %get-tuple-element.58, f32[30,4,4]{0,2,1:T(4,128)S(1)} %neg.7, f32[30,4,4]{0,2,1:T(4,128)S(1)} %get-tuple-element.44), kind=kOutput, calls=%fused_computation.20 | convolution fusion | flops 47208064 | bytes 2102912 | tf_op jit(solution)/shard_map/jab,jan->bn/dot_general | solution.py:71
  163.6 0.0 copy-start.1
  163.6 0.2 fusion.48
  163.8 9.0 %psum.31 = f32[8,8]{1,0:T(8,128)S(1)} all-reduce(f32[8,8]{1,0:T(8,128)S(1)} %fusion.48), channel_id=1, replica_groups=mesh['row'=4,'col'=4,'grp'=2] {'row'}, use_global_device_ids=true, to_apply=%region_6.7 | all-reduce | flops 64 | bytes 512 | tf_op jit(solution)/shard_map/psum | solution.py:83
  172.8 0.1 add_bitcast_fusion.2
  172.9 0.6 pad_maximum_fusion.2
  173.5 0.6 pad_maximum_fusion
  174.1 0.0 copy-done.1
  (27 shorter events, 0.3 us)
Async XLA Ops:
  7.2 110.4 %all-reduce.2.cloned.1.call-start = ((), (), s32[]{:S(2)}) async-start(), calls=%async_computation | async-start | bytes 131072 | tf_op jit(solution)/shard_map/psum | solution.py:121
  20.2 97.4 %copy-start = (f32[30,8,2048]{2,1,0:T(8,128)S(1)}, f32[30,8,2048]{2,1,0:T(8,128)}, u32[]{:S(2)}) copy-start(f32[30,8,2048]{2,1,0:T(8,128)} %param.6) | copy-start | bytes 5898244
  61.8 0.6 copy-start.3
  117.6 22.0 %copy-start.2 = (f32[8,2048]{1,0:T(8,128)S(1)}, f32[8,2048]{1,0:T(8,128)}, u32[]{:S(2)}) copy-start(f32[8,2048]{1,0:T(8,128)} %all-reduce.2.cloned.1.call-done) | copy-start | bytes 196612
  163.6 10.5 %copy-start.1 = (f32[8,2048]{1,0:T(8,128)}, f32[8,2048]{1,0:T(8,128)S(1)}, u32[]{:S(2)}) copy-start(f32[8,2048]{1,0:T(8,128)S(1)} %fusion.11) | copy-start | bytes 196612
Sparse Core Ops, SparseCore 0:
  62.6 54.9 all-reduce.1
where the time goes:
time: 181 us
  waiting for transfers between devices  55.2 us (30%)
  blocking collectives  49.3 us (27%)
  other arithmetic  42.3 us (23%)
  matrix products  18.1 us (10%)
  between operations  14.1 us (8%)
    psum x1, waiting for transfers between devices, local(): initial = direction - lax.psum(scattered, ('col', 'grp'))  55.1 us
    another operation x4, other arithmetic  38.6 us
    psum x1, blocking collectives, row_first_sum(): return lax.psum(value, 'row')  16.2 us
    psum x1, blocking collectives, row_second_sum(): return lax.psum(value, 'row')  14.3 us
    dot_general x2, matrix products, project(): return jnp.einsum('jan,bn->jab', krylov_basis, field, precision=highest)  10.5 us
    all_gather x1, blocking collectives, local(): portion = lax.all_gather(packed, 'row', axis=1, tiled=True)  9.71 us
    psum x1, blocking collectives, row_norm_sum(): return lax.psum(value, 'row')  9.05 us
    dot_general x2, matrix products, subtract(): jnp.einsum('jab,jan->bn', mixing, krylov_basis, precision=highest)  4.91 us
  transfers between devices with their start and end apart: 1, of which 1 were waited for; matrix products, arithmetic and copies ran while one was open for 0% of the time, Pallas kernels for 0%

commit v1 on v0

v1 whole, which is shorter than its diff:
```python
import functools
import math

import jax
import jax.numpy as jnp
from jax import lax
from jax.experimental import pallas as pl
from jax.experimental.pallas import tpu as pltpu
from jax.sharding import PartitionSpec as P

SIN = (1.4142087387611353, -0.23567610974963038, 0.011746768515409164, -0.00025966094816487484)
COS = (
    1.4142134959114503,
    -0.7071054319872576,
    0.05892118073562594,
    -0.0019591901398600675,
    3.274008676623641e-05,
)
PI_HIGH = 3.1415863037109375
PI_LOW = math.pi - PI_HIGH
f32 = jnp.float32
bf16 = jnp.bfloat16
MESH = pl.DeviceIdType.MESH


def poly(u, coefs):
    value = jnp.full_like(u, coefs[-1])
    for c in coefs[-2::-1]:
        value = value * u + c
    return value


def green(squared):
    inverse = jnp.where(squared > 0.5, lax.rsqrt(squared), 0.0)
    distance = squared * inverse
    turns = jnp.round(distance * (1.0 / math.pi))
    r = (distance - turns * PI_HIGH) - turns * PI_LOW
    u = r * r
    s = r * poly(u, SIN)
    scaled = s * inverse
    real_part = inverse - s * scaled
    imag_part = scaled * poly(u, COS)
    return real_part.astype(bf16), imag_part.astype(bf16)


def features(sites, is_source):
    x = sites.astype(f32)
    norm = jnp.sum(x * x, axis=0, keepdims=True)
    high = jnp.floor(norm * (1.0 / 256.0)) * 256.0
    low = norm - high
    one = jnp.ones_like(norm)
    if is_source:
        parts = [-2.0 * x, one, one, high, low, jnp.zeros_like(norm)]
    else:
        parts = [x, high, low, one, one, jnp.zeros_like(norm)]
    return jnp.concatenate(parts, 0)


def split(x):
    high = x.astype(bf16)
    return high, (x - high.astype(f32)).astype(bf16)


def turn_rows(x):
    half = x.shape[0] // 2
    return jnp.concatenate([x[half:], -x[:half]], 0)


def kernel(
    dims, table_ref, basis_hbm, lattice_ref, index_ref, coef_ref, gram_ref, new_ref,
    basis, high, low, gath, tgt, partial, landed, field, coef1, coef2, grams,
    copy_sem, send1, recv1, send2, recv2, send3, recv3, send4, recv4, send5, recv5, send6, recv6,
):
    R, C, G, blk, tile, points, nb, ch, table = dims
    parts = C * G
    T = parts * blk
    K = nb * ch
    KP = coef1.shape[2]
    row, col, grp = lax.axis_index("row"), lax.axis_index("col"), lax.axis_index("grp")
    me = col * G + grp
    load = pltpu.make_async_copy(basis_hbm, basis, copy_sem)
    load.start()

    barrier = pltpu.get_barrier_semaphore()
    for k in range(1, R):
        pl.semaphore_signal(
            barrier, inc=1, device_id={"row": lax.rem(row + k, R)}, device_id_type=MESH
        )
    for k in range(1, parts):
        other = lax.rem(me + k, parts)
        pl.semaphore_signal(
            barrier, inc=1, device_id={"col": other // G, "grp": lax.rem(other, G)},
            device_id_type=MESH,
        )

    own = pl.ds(pl.multiple_of(me * blk, blk), blk)
    index = index_ref[:, own]
    strength = jnp.zeros(index.shape, f32)
    for entry in range(table):
        strength = jnp.where(index == entry, table_ref[entry], strength)
    sources = features(lattice_ref[:, own], True)
    zeros = jnp.zeros((8, T), f32)
    tgt[...] = jnp.concatenate([features(lattice_ref[...], False), zeros], 0).astype(bf16)
    load.wait()
    weighted = basis[K - ch:, own] * strength
    gath[pl.ds(row, 1)] = jnp.concatenate([weighted, sources], 0).astype(bf16)[None]
    step = math.gcd(T, 512)

    @pl.loop(0, T // step)
    def _(i):
        at = pl.ds(pl.multiple_of(i * step, step), step)
        b_high, b_low = split(basis[:, at])
        high[:, at] = b_high
        low[:, at] = b_low

    pl.semaphore_wait(barrier, R - 1 + parts - 1)

    def row_copy(ref, sends, recvs, slot, peer):
        return pltpu.make_async_remote_copy(
            src_ref=ref.at[slot], dst_ref=ref.at[slot], send_sem=sends.at[peer],
            recv_sem=recvs.at[slot], device_id={"row": peer}, device_id_type=MESH,
        )

    def row_send(ref, sends, recvs):
        for k in range(1, R):
            row_copy(ref, sends, recvs, row, lax.rem(row + k, R)).start()

    def row_wait(ref, sends, recvs):
        for k in range(1, R):
            peer = lax.rem(row + k, R)
            copy = row_copy(ref, sends, recvs, peer, peer)
            copy.wait_recv()
            copy.wait_send()

    row_send(gath, send1, recv1)

    def scatter(chunk, part):
        block = gath[pl.ds(chunk, 1)][0].astype(f32)
        weights = block[:8]
        direct = weights.astype(bf16)
        turned = jnp.concatenate([-weights[4:], weights[:4]], 0).astype(bf16)
        sites = jnp.concatenate([block[8:], jnp.zeros((8, blk), f32)], 0).T.astype(bf16)
        at = pl.ds(pl.multiple_of(part * blk, blk), blk)
        targets = tgt[:, at]
        squared = jnp.dot(sites, targets, preferred_element_type=f32)
        real_part, imag_part = green(squared)
        return jnp.dot(direct, real_part, preferred_element_type=f32) + jnp.dot(
            turned, imag_part, preferred_element_type=f32
        )

    def target_of(k):
        left = parts - 1 - k
        to_col = lax.rem(col + left // G, C)
        to_grp = lax.rem(grp + left, G)
        return to_col, to_grp

    @pl.loop(0, parts)
    def _(k):
        to_col, to_grp = target_of(k)
        part = to_col * G + to_grp
        partial[pl.ds(part, 1)] = scatter(row, part)[None]

    row_wait(gath, send1, recv1)

    def part_send(part, to_col, to_grp):
        return pltpu.make_async_remote_copy(
            src_ref=partial.at[part], dst_ref=landed.at[me], send_sem=send2.at[part],
            recv_sem=recv2.at[me], device_id={"col": to_col, "grp": to_grp}, device_id_type=MESH,
        )

    @pl.loop(0, parts)
    def _(k):
        to_col, to_grp = target_of(k)
        part = to_col * G + to_grp

        def more(q, total):
            return total + scatter(lax.rem(row + q, R), part)

        total = lax.fori_loop(1, R, more, partial[pl.ds(part, 1)][0])
        partial[pl.ds(part, 1)] = total[None]

        @pl.when(k < parts - 1)
        def _():
            part_send(part, to_col, to_grp).start()

    total = basis[K - ch:, own] - partial[pl.ds(me, 1)][0]
    for k in range(1, parts):
        other = lax.rem(me + k, parts)
        copy = pltpu.make_async_remote_copy(
            src_ref=partial.at[other], dst_ref=landed.at[other], send_sem=send2.at[other],
            recv_sem=recv2.at[other], device_id={"col": other // G, "grp": lax.rem(other, G)},
            device_id_type=MESH,
        )
        copy.wait_recv()
        copy.wait_send()
        total = total - landed[pl.ds(other, 1)][0]
    field[:, own] = total

    def field_copy(slot, to):
        at = pl.ds(pl.multiple_of(slot * blk, blk), blk)
        return pltpu.make_async_remote_copy(
            src_ref=field.at[:, at], dst_ref=field.at[:, at], send_sem=send3.at[to],
            recv_sem=recv3.at[slot], device_id={"col": to // G, "grp": lax.rem(to, G)},
            device_id_type=MESH,
        )

    for k in range(1, parts):
        field_copy(me, lax.rem(me + k, parts)).start()
    for k in range(1, parts):
        other = lax.rem(me + k, parts)
        copy = field_copy(other, other)
        copy.wait_recv()
        copy.wait_send()

    lanes = (((1,), (1,)), ((), ()))

    def product(x, numbers):
        x_high, x_low = split(x)
        stacked = jnp.concatenate([x_high.astype(f32), x_low.astype(f32)], 0).astype(bf16)
        out = lax.dot_general(stacked, high[...], numbers, preferred_element_type=f32)
        out = out + lax.dot_general(stacked, low[...], numbers, preferred_element_type=f32)
        return out[:8] + out[8:]

    def project(x, coef, sends, recvs):
        coef[pl.ds(row, 1), :, :K] = product(x, lanes)[None]
        if KP > K:
            coef[pl.ds(row, 1), :, K:] = jnp.zeros((1, ch, KP - K), f32)
        row_send(coef, sends, recvs)
        row_wait(coef, sends, recvs)
        sums = jnp.sum(coef[...], 0) * (1.0 / points)
        turned = turn_rows(sums)
        lane = lax.broadcasted_iota(jnp.int32, turned.shape, 1)
        half = ch // 2
        turned = jnp.where(
            lane % ch < half, pltpu.roll(turned, KP - half, 1), -pltpu.roll(turned, half, 1)
        )
        return sums + turned

    def subtract(x, mixing):
        return x - product(mixing[:, :K], (((1,), (0,)), ((), ())))

    initial = field[...]
    once_coef = project(initial, coef1, send4, recv4)
    once = subtract(initial, once_coef)
    twice_coef = project(once, coef2, send5, recv5)
    new_block = subtract(once, twice_coef)
    coef_ref[...] = once_coef + twice_coef
    new_ref[...] = new_block
    n_high, n_low = split(new_block)
    gram = (
        lax.dot_general(n_high, n_high, lanes, preferred_element_type=f32)
        + lax.dot_general(n_high, n_low, lanes, preferred_element_type=f32)
        + lax.dot_general(n_low, n_high, lanes, preferred_element_type=f32)
    )
    grams[pl.ds(row, 1)] = jnp.zeros((1,) + grams.shape[1:], f32)
    grams[pl.ds(row, 1), :, :ch] = gram[None]
    row_send(grams, send6, recv6)
    row_wait(grams, send6, recv6)
    gram_ref[...] = jnp.sum(grams[...], 0) * (1.0 / points)


def local(krylov_basis, lattice, strength_index, strength_table):
    R, C, G = (lax.axis_size(a) for a in ("row", "col", "grp"))
    nb, ch, T = krylov_basis.shape
    parts = C * G
    blk = T // parts
    K = nb * ch
    KP = -(-K // 128) * 128
    table = strength_table.shape[0]
    dims = (R, C, G, blk, blk, T * R, nb, ch, table)
    vmem = pl.BlockSpec(memory_space=pltpu.VMEM)
    dma = pltpu.SemaphoreType.DMA
    coefs, gram, new_block = pl.pallas_call(
        functools.partial(kernel, dims),
        out_shape=(
            jax.ShapeDtypeStruct((ch, KP), f32),
            jax.ShapeDtypeStruct((ch, 128), f32),
            jax.ShapeDtypeStruct((ch, T), f32),
        ),
        in_specs=[
            pl.BlockSpec(memory_space=pltpu.SMEM), pl.BlockSpec(memory_space=pl.ANY), vmem, vmem,
        ],
        out_specs=(vmem, vmem, vmem),
        scratch_shapes=[
            pltpu.VMEM((K, T), f32),
            pltpu.VMEM((K, T), bf16),
            pltpu.VMEM((K, T), bf16),
            pltpu.VMEM((R, 16, blk), bf16),
            pltpu.VMEM((16, T), bf16),
            pltpu.VMEM((parts, ch, blk), f32),
            pltpu.VMEM((parts, ch, blk), f32),
            pltpu.VMEM((ch, T), f32),
            pltpu.VMEM((R, ch, KP), f32),
            pltpu.VMEM((R, ch, KP), f32),
            pltpu.VMEM((R, ch, 128), f32),
            dma,
            dma((R,)), dma((R,)),
            dma((parts,)), dma((parts,)),
            dma((parts,)), dma((parts,)),
            dma((R,)), dma((R,)),
            dma((R,)), dma((R,)),
            dma((R,)), dma((R,)),
        ],
        compiler_params=pltpu.CompilerParams(
            collective_id=0, has_side_effects=True, vmem_limit_bytes=48 * 1024 * 1024
        ),
        name="foldy_step",
    )(strength_table, krylov_basis.reshape(K, T), lattice, strength_index.reshape(1, T))
    half = ch // 2
    mixing = coefs[:, :K].reshape(2, half, nb, ch)[..., :half]
    hessenberg = mixing.transpose(2, 0, 3, 1)
    g = gram[:, :ch]
    block_gram = jnp.stack(
        [g[:half, :half] + g[half:, half:], g[:half, half:] - g[half:, :half]], 0
    )
    return (new_block, hessenberg, block_gram)


def solution(mesh):
    in_specs = (P(None, None, "row"), P(None, "row"), P("row"), P())
    out_specs = (P(None, "row"), P(), P())
    return jax.shard_map(local, mesh=mesh, in_specs=in_specs, out_specs=out_specs, check_vma=False)
```

time: 181 us -> 49.1 us (0.27)
  waiting for transfers between devices: 55.2 us -> 0 us
  blocking collectives: 49.3 us -> 0 us
  Pallas kernels: 0 us -> 42.4 us
  other arithmetic: 42.3 us -> 0.67 us
  matrix products: 18.1 us -> 0 us
  between operations: 14.1 us -> 0.67 us
  local copies, waits for them, and re-layouts: 1.66 us -> 5.11 us
    psum x1 -> x0, waiting for transfers between devices: 55.1 us -> none  [local(): initial = direction - lax.psum(scattered, ('col', 'grp'))]
    pallas_call x0 -> x1, Pallas kernels: none -> 42.4 us  [local(): pl.pallas_call(functools.partial(kernel, dims), out_shape=(jax.ShapeDtype...]
    psum x3 -> x0, blocking collectives: 39.6 us -> none  [the longest x1 16.2 us: row_first_sum(): return lax.psum(value, 'row')]
    another operation x8 -> x2, other arithmetic: 39.9 us -> 0.67 us  [local(): jnp.stack([g[:half, :half] + g[half:, half:], g[:half, half:] - g[half:,...]
    dot_general x9 -> x0, matrix products: 18.1 us -> none  [the longest x2 10.5 us: project(): return jnp.einsum('jan,bn->jab', krylov_basis, field, precision=highest)]
    all_gather x1 -> x0, blocking collectives: 9.71 us -> none  [local(): portion = lax.all_gather(packed, 'row', axis=1, tiled=True)]
    unnamed x8 -> x10, local copies, waits for them, and re-layouts: 0.64 us -> 5 us
  transfers between devices with their start and end apart: 1 -> 0, of which waited for: 1 -> 0; matrix products, arithmetic and copies ran while one was open for 0% -> 0% of each run, Pallas kernels for 0% -> 0%
where the time goes in v1:
time: 49.1 us; the launch traced here: 48.9 us
  Pallas kernels  42.4 us (86%)
  local copies, waits for them, and re-layouts  5.11 us (10%)
  other arithmetic  0.67 us (1%)
  between operations  0.67 us (1%)
    pallas_call x1, Pallas kernels, local(): pl.pallas_call(functools.partial(kernel, dims), out_shape=(jax.ShapeDtype...  42.4 us
    unnamed x10, local copies, waits for them, and re-layouts  5 us

profile of v1, /device:TPU:0, one launch (start us, length us, event | category | flops | bytes accessed | tf_op | source)
XLA Modules:
  0.0 48.9 jit_solution(10965496899777202601)
XLA Ops:
  0.6 0.0 copy-start
  0.6 1.5 %copy-done = f32[30,8,2048]{2,1,0:T(8,128)S(1)} copy-done((f32[30,8,2048]{2,1,0:T(8,128)S(1)}, f32[30,8,2048]{2,1,0:T(8,128)}, u32[]{:S(2)}) %copy-start) | copy-done | bytes 1966104
  2.2 0.0 copy-start.1
  2.2 0.8 %copy-done.1 = s32[3,2048]{1,0:T(4,128)S(1)} copy-done((s32[3,2048]{1,0:T(4,128)S(1)}, s32[3,2048]{1,0:T(4,128)}, u32[]{:S(2)}) %copy-start.1) | copy-done | bytes 24600
  2.9 0.0 copy-start.2
  2.9 0.7 %copy-done.2 = s32[2048]{0:T(1024)S(1)} copy-done((s32[2048]{0:T(1024)S(1)}, s32[2048]{0:T(1024)}, u32[]{:S(2)}) %copy-start.2) | copy-done | bytes 8216
  3.6 0.0 copy-start.3
  3.6 0.7 %copy-done.3 = f32[16]{0:T(128)S(1)} copy-done((f32[16]{0:T(128)S(1)}, f32[16]{0:T(128)}, u32[]{:S(2)}) %copy-start.3) | copy-done | bytes 88
  4.3 42.4 %foldy_step.1 = (f32[8,256]{1,0:T(8,128)S(1)}, f32[8,128]{1,0:T(8,128)S(1)}, f32[8,2048]{1,0:T(8,128)S(1)}) custom-call(f32[16]{0:T(128)S(1)} %copy-done.3, f32[240,2048]{1,0:T(8,128)S(1)} %bitcast.9, s32[3,2048]{1,0:T(4,128)S(1)} %copy-done.1, s32[1,2048]{1,0:T(1,128)S(1)} %bitcast.10), custom_call_target="tpu_custom_call" | custom-call | tf_op jit(solution)/shard_map/foldy_step/pallas_call | solution.py:273
  46.7 0.1 add_bitcast_fusion
  46.8 0.6 %pad_maximum_fusion = f32[2,4,4]{2,1,0:T(4,128)} fusion(f32[1,4,4]{2,1,0:T(4,128)S(1)} %get-tuple-element.13, f32[1,4,4]{2,1,0:T(4,128)S(1)} %get-tuple-element.12), kind=kLoop, calls=%fused_computation.1 | loop fusion | flops 32 | bytes 256 | tf_op jit(solution)/shard_map/stack | solution.py:313
  47.4 0.1 reshape.17
  47.5 0.7 %copy.8 = f32[30,2,4,4]{0,3,2,1:T(4,128)} copy(f32[30,2,4,4]{2,0,3,1:T(8,128)S(1)} %slice_bitcast_fusion) | data formatting | bytes 7680
  48.2 0.6 %copy.10 = f32[8,2048]{1,0:T(8,128)} copy(f32[8,2048]{1,0:T(8,128)S(1)} %get-tuple-element.17) | data formatting | bytes 131072
  (1 shorter events, 0.0 us)
Async XLA Ops:
  0.6 1.5 %copy-start = (f32[30,8,2048]{2,1,0:T(8,128)S(1)}, f32[30,8,2048]{2,1,0:T(8,128)}, u32[]{:S(2)}) copy-start(f32[30,8,2048]{2,1,0:T(8,128)} %param.4) | copy-start | bytes 5898244
  2.2 0.8 %copy-start.1 = (s32[3,2048]{1,0:T(4,128)S(1)}, s32[3,2048]{1,0:T(4,128)}, u32[]{:S(2)}) copy-start(s32[3,2048]{1,0:T(4,128)} %lattice_ref.1) | copy-start | bytes 73732
  2.9 0.7 %copy-start.2 = (s32[2048]{0:T(1024)S(1)}, s32[2048]{0:T(1024)}, u32[]{:S(2)}) copy-start(s32[2048]{0:T(1024)} %param.6) | copy-start | bytes 24580
  3.6 0.7 %copy-start.3 = (f32[16]{0:T(128)S(1)}, f32[16]{0:T(128)}, u32[]{:S(2)}) copy-start(f32[16]{0:T(128)} %table_ref.1) | copy-start | bytes 196

commit v2 on v1

v2 whole, which is shorter than its diff:
```python
import functools
import math

import jax
import jax.numpy as jnp
from jax import lax
from jax.experimental import pallas as pl
from jax.experimental.pallas import tpu as pltpu
from jax.sharding import PartitionSpec as P

SIN = (
    4.44286778433447,
    -7.307438665833745,
    3.5947423983311806,
    -0.784252203260472,
)
COS = (
    1.4142134959114503,
    -6.978850883575629,
    5.7394586581074964,
    -1.883544228620758,
    0.3106553287502758,
)
f32 = jnp.float32
bf16 = jnp.bfloat16
MESH = pl.DeviceIdType.MESH


def poly(u, coefs):
    value = jnp.full_like(u, coefs[-1])
    for c in coefs[-2::-1]:
        value = value * u + c
    return value


def green(squared, masked):
    inverse = lax.rsqrt(squared)
    if masked:
        inverse = jnp.where(squared > 0.5, inverse, 0.0)
    half_turns = squared * inverse * (1.0 / math.pi)
    r = half_turns - jnp.round(half_turns)
    u = r * r
    s = r * poly(u, SIN)
    scaled = s * inverse
    real_part = inverse - s * scaled
    imag_part = scaled * poly(u, COS)
    return real_part.astype(bf16), imag_part.astype(bf16)


def features(sites, is_source):
    x = sites.astype(f32)
    norm = jnp.sum(x * x, axis=0, keepdims=True)
    high = jnp.floor(norm * (1.0 / 256.0)) * 256.0
    low = norm - high
    one = jnp.ones_like(norm)
    if is_source:
        parts = [-2.0 * x, one, one, high, low, jnp.zeros_like(norm)]
    else:
        parts = [x, high, low, one, one, jnp.zeros_like(norm)]
    return jnp.concatenate(parts, 0)


def split(x):
    high = x.astype(bf16)
    return high, (x - high.astype(f32)).astype(bf16)


def turn_rows(x):
    half = x.shape[0] // 2
    return jnp.concatenate([x[half:], -x[:half]], 0)


def turn_lanes(x, ch):
    half = ch // 2
    lane = lax.broadcasted_iota(jnp.int32, x.shape, 1)
    return jnp.where(
        lane % ch < half, pltpu.roll(x, x.shape[1] - half, 1), -pltpu.roll(x, half, 1)
    )


def lift(x):
    return x + turn_lanes(turn_rows(x), x.shape[0])


def dot(x, y, numbers=(((1,), (0,)), ((), ()))):
    return lax.dot_general(
        x, y, numbers, precision=lax.Precision.HIGHEST, preferred_element_type=f32
    )


lanes = (((1,), (1,)), ((), ()))


def kernel(
    dims, table_hbm, basis_hbm, lattice_hbm, index_hbm, coef_ref, gram_ref, new_ref,
    table_ref, direction, lattice_ref, index_ref,
    basis, high, low, overlap, halves, metric, gath, tgt, partial, landed, field, coef,
    copy_sem, send1, recv1, send2, recv2, send3, recv3, send4, recv4, send5, recv5,
):
    R, C, G, blk, points, nb, ch, table = dims
    parts = C * G
    T = parts * blk
    K = nb * ch
    KP = basis.shape[0]
    half = ch // 2
    blocks = KP // ch
    planes = KP // 128
    row, col, grp = lax.axis_index("row"), lax.axis_index("col"), lax.axis_index("grp")
    me = col * G + grp
    own = pl.ds(pl.multiple_of(me * blk, blk), blk)
    loads = [
        pltpu.make_async_copy(lattice_hbm, lattice_ref, copy_sem.at[0]),
        pltpu.make_async_copy(index_hbm.at[:, own], index_ref, copy_sem.at[1]),
        pltpu.make_async_copy(basis_hbm.at[pl.ds(K - ch, ch), own], direction, copy_sem.at[2]),
        pltpu.make_async_copy(table_hbm, table_ref, copy_sem.at[3]),
        pltpu.make_async_copy(basis_hbm, basis.at[pl.ds(0, K)], copy_sem.at[4]),
    ]
    for load in loads:
        load.start()

    barrier = pltpu.get_barrier_semaphore()
    for k in range(1, R):
        pl.semaphore_signal(
            barrier, inc=1, device_id={"row": lax.rem(row + k, R)}, device_id_type=MESH
        )
    for k in range(1, parts):
        other = lax.rem(me + k, parts)
        pl.semaphore_signal(
            barrier, inc=1, device_id={"col": other // G, "grp": lax.rem(other, G)},
            device_id_type=MESH,
        )

    if KP > K:
        basis[K:] = jnp.zeros((KP - K, T), f32)
    overlap[...] = jnp.zeros_like(overlap)
    for load in loads[:4]:
        load.wait()
    index = index_ref[...]
    strength = jnp.zeros(index.shape, f32)
    for entry in range(table):
        strength = jnp.where(index == entry, table_ref[entry], strength)
    sources = features(lattice_ref[:, own], True)
    gath[pl.ds(row, 1)] = jnp.concatenate([direction[...] * strength, sources], 0).astype(bf16)[
        None
    ]
    zeros = jnp.zeros((8, T), f32)
    tgt[...] = jnp.concatenate([features(lattice_ref[...], False), zeros], 0).astype(bf16)
    pl.semaphore_wait(barrier, R - 1 + parts - 1)

    def row_copy(ref, sends, recvs, slot, peer):
        return pltpu.make_async_remote_copy(
            src_ref=ref.at[slot], dst_ref=ref.at[slot], send_sem=sends.at[peer],
            recv_sem=recvs.at[slot], device_id={"row": peer}, device_id_type=MESH,
        )

    def row_send(ref, sends, recvs):
        for k in range(1, R):
            row_copy(ref, sends, recvs, row, lax.rem(row + k, R)).start()

    def row_wait(ref, sends, recvs):
        for k in range(1, R):
            peer = lax.rem(row + k, R)
            copy = row_copy(ref, sends, recvs, peer, peer)
            copy.wait_recv()
            copy.wait_send()

    row_send(gath, send1, recv1)
    loads[4].wait()

    def scatter(chunk, part, masked=False):
        block = gath[pl.ds(chunk, 1)][0].astype(f32)
        weights = block[:8]
        direct = weights.astype(bf16)
        turned = jnp.concatenate([-weights[4:], weights[:4]], 0).astype(bf16)
        sites = jnp.concatenate([block[8:], jnp.zeros((8, blk), f32)], 0).T.astype(bf16)
        at = pl.ds(pl.multiple_of(part * blk, blk), blk)
        targets = tgt[:, at]
        squared = jnp.dot(sites, targets, preferred_element_type=f32)
        real_part, imag_part = green(squared, masked)
        return jnp.dot(direct, real_part, preferred_element_type=f32) + jnp.dot(
            turned, imag_part, preferred_element_type=f32
        )

    def target_of(k):
        left = parts - 1 - k
        to_col = lax.rem(col + left // G, C)
        to_grp = lax.rem(grp + left, G)
        return to_col, to_grp

    def first_part(part, masked):
        at = pl.ds(pl.multiple_of(part * blk, blk), blk)
        b_high, b_low = split(basis[:, at])
        high[:, at] = b_high
        low[:, at] = b_low
        products = lax.dot_general(
            jnp.concatenate([b_high, b_low, b_high], 1),
            jnp.concatenate([b_high, b_high, b_low], 1),
            lanes, preferred_element_type=f32,
        )
        for p in range(planes):
            overlap[p] += products[:, p * 128:(p + 1) * 128]
        partial[pl.ds(part, 1)] = scatter(row, part, masked)[None]

    @pl.loop(0, parts - 1)
    def _(k):
        to_col, to_grp = target_of(k)
        first_part(to_col * G + to_grp, False)

    first_part(me, True)

    for a in range(half):
        for p in range(planes):
            upper = overlap[p, pl.ds(a, blocks, stride=ch), :]
            lower = overlap[p, pl.ds(a + half, blocks, stride=ch), :]
            halves[pl.ds(row, 1), pl.ds(a * blocks, blocks), p * 128:(p + 1) * 128] = (
                upper + turn_lanes(lower, ch)
            )[None]
    row_wait(gath, send1, recv1)
    row_send(halves, send5, recv5)

    def part_send(part, to_col, to_grp):
        return pltpu.make_async_remote_copy(
            src_ref=partial.at[part], dst_ref=landed.at[me], send_sem=send2.at[part],
            recv_sem=recv2.at[me], device_id={"col": to_col, "grp": to_grp}, device_id_type=MESH,
        )

    @pl.loop(0, parts)
    def _(k):
        to_col, to_grp = target_of(k)
        part = to_col * G + to_grp

        def more(q, total):
            return total + scatter(lax.rem(row + q, R), part)

        total = lax.fori_loop(1, R, more, partial[pl.ds(part, 1)][0], unroll=R <= 4)
        partial[pl.ds(part, 1)] = total[None]

        @pl.when(k < parts - 1)
        def _():
            part_send(part, to_col, to_grp).start()

    total = partial[pl.ds(me, 1)][0]
    for k in range(1, parts):
        other = lax.rem(me + k, parts)
        copy = pltpu.make_async_remote_copy(
            src_ref=partial.at[other], dst_ref=landed.at[other], send_sem=send2.at[other],
            recv_sem=recv2.at[other], device_id={"col": other // G, "grp": lax.rem(other, G)},
            device_id_type=MESH,
        )
        copy.wait_recv()
        copy.wait_send()
        total = total + landed[pl.ds(other, 1)][0]
    field[:, own] = total

    def field_copy(slot, to):
        at = pl.ds(pl.multiple_of(slot * blk, blk), blk)
        return pltpu.make_async_remote_copy(
            src_ref=field.at[:, at], dst_ref=field.at[:, at], send_sem=send3.at[to],
            recv_sem=recv3.at[slot], device_id={"col": to // G, "grp": lax.rem(to, G)},
            device_id_type=MESH,
        )

    for k in range(1, parts):
        field_copy(me, lax.rem(me + k, parts)).start()
    for k in range(1, parts):
        other = lax.rem(me + k, parts)
        copy = field_copy(other, other)
        copy.wait_recv()
        copy.wait_send()

    def product(x, numbers):
        x_high, x_low = split(x)
        stacked = jnp.concatenate([x_high.astype(f32), x_low.astype(f32)], 0).astype(bf16)
        out = lax.dot_general(stacked, high[...], numbers, preferred_element_type=f32)
        out = out + lax.dot_general(stacked, low[...], numbers, preferred_element_type=f32)
        return out[:8] + out[8:]

    scattered = field[...]
    coef[pl.ds(row, 1), :, :KP] = product(scattered, lanes)[None]
    coef[pl.ds(row, 1), :, KP:] = jnp.zeros((1, ch, 128), f32)
    coef[pl.ds(row, 1), :, pl.ds(KP, ch)] = dot(scattered, scattered, lanes)[None]
    row_send(coef, send4, recv4)

    scale = 1.0 / points
    row_wait(halves, send5, recv5)
    for a in range(half):
        rows = jnp.sum(halves[:, pl.ds(a * blocks, blocks), :], 0) * scale
        turned = -turn_lanes(rows, ch)
        for p in range(planes):
            at = slice(p * 128, (p + 1) * 128)
            metric[p, pl.ds(a, blocks, stride=ch), :] = rows[:, at]
            metric[p, pl.ds(a + half, blocks, stride=ch), :] = turned[:, at]
    row_wait(coef, send4, recv4)
    sums = jnp.sum(coef[...], 0) * scale
    mixed = lift(sums[:, :KP])
    self_gram = lift(sums[:, KP:])[:, :ch]
    full = jnp.concatenate([metric[p] for p in range(planes)], 1)
    once = full[K - ch:K] - mixed
    twice = once - dot(once, full)
    both = once + twice
    coef_ref[...] = both
    at_row = lax.broadcasted_iota(jnp.int32, both.shape, 0)
    at_lane = lax.broadcasted_iota(jnp.int32, both.shape, 1)
    change = both - jnp.where(at_lane == at_row + (K - ch), 1.0, 0.0)
    new_ref[...] = -(scattered + product(change, (((1,), (0,)), ((), ()))))
    cross = dot(mixed, change, lanes)
    cross_t = dot(change, mixed, lanes)
    gram_ref[...] = jnp.zeros_like(gram_ref)
    gram_ref[:, :ch] = self_gram + cross + cross_t + dot(
        dot(change, full), change, lanes
    )


def local(krylov_basis, lattice, strength_index, strength_table):
    R, C, G = (lax.axis_size(a) for a in ("row", "col", "grp"))
    nb, ch, T = krylov_basis.shape
    parts = C * G
    blk = T // parts
    K = nb * ch
    KP = -(-K // 128) * 128
    table = strength_table.shape[0]
    dims = (R, C, G, blk, T * R, nb, ch, table)
    vmem = pl.BlockSpec(memory_space=pltpu.VMEM)
    hbm = pl.BlockSpec(memory_space=pltpu.HBM)
    dma = pltpu.SemaphoreType.DMA
    coefs, gram, new_block = pl.pallas_call(
        functools.partial(kernel, dims),
        out_shape=(
            jax.ShapeDtypeStruct((ch, KP), f32),
            jax.ShapeDtypeStruct((ch, 128), f32),
            jax.ShapeDtypeStruct((ch, T), f32),
        ),
        in_specs=[hbm, hbm, hbm, hbm],
        out_specs=(vmem, vmem, vmem),
        scratch_shapes=[
            pltpu.SMEM((table,), f32),
            pltpu.VMEM((ch, blk), f32),
            pltpu.VMEM((3, T), jnp.int32),
            pltpu.VMEM((1, blk), jnp.int32),
            pltpu.VMEM((KP, T), f32),
            pltpu.VMEM((KP, T), bf16),
            pltpu.VMEM((KP, T), bf16),
            pltpu.VMEM((KP // 128, KP, 128), f32),
            pltpu.VMEM((R, KP // 2, KP), f32),
            pltpu.VMEM((KP // 128, KP, 128), f32),
            pltpu.VMEM((R, 16, blk), bf16),
            pltpu.VMEM((16, T), bf16),
            pltpu.VMEM((parts, ch, blk), f32),
            pltpu.VMEM((parts, ch, blk), f32),
            pltpu.VMEM((ch, T), f32),
            pltpu.VMEM((R, ch, KP + 128), f32),
            dma((5,)),
            dma((R,)), dma((R,)),
            dma((parts,)), dma((parts,)),
            dma((parts,)), dma((parts,)),
            dma((R,)), dma((R,)),
            dma((R,)), dma((R,)),
        ],
        compiler_params=pltpu.CompilerParams(
            collective_id=0, has_side_effects=True, vmem_limit_bytes=48 * 1024 * 1024
        ),
        name="foldy_step",
    )(strength_table, krylov_basis.reshape(K, T), lattice, strength_index.reshape(1, T))
    half = ch // 2
    mixing = coefs[:, :K].reshape(2, half, nb, ch)[..., :half]
    hessenberg = mixing.transpose(2, 0, 3, 1)
    block_gram = jnp.stack([gram[:half, :half], gram[:half, half:ch]], 0)
    return (new_block, hessenberg, block_gram)


def solution(mesh):
    in_specs = (P(None, None, "row"), P(None, "row"), P("row"), P())
    out_specs = (P(None, "row"), P(), P())
    return jax.shard_map(local, mesh=mesh, in_specs=in_specs, out_specs=out_specs, check_vma=False)
```

time: 49.1 us -> 36.4 us (0.74)
  Pallas kernels: 42.4 us -> 29.7 us
    pallas_call x1, Pallas kernels: 42.4 us -> 29.7 us  [local(): pl.pallas_call(functools.partial(kernel, dims), out_shape=(jax.ShapeDtype...]
where the time goes in v2:
time: 36.4 us; the launch traced here: 36.1 us
  Pallas kernels  29.7 us (82%)
  local copies, waits for them, and re-layouts  5.18 us (14%)
  between operations  0.67 us (2%)
  other arithmetic  0.6 us (2%)
    pallas_call x1, Pallas kernels, local(): pl.pallas_call(functools.partial(kernel, dims), out_shape=(jax.ShapeDtype...  29.7 us
    unnamed x10, local copies, waits for them, and re-layouts  5 us

profile of v2, /device:TPU:0, one launch (start us, length us, event | category | flops | bytes accessed | tf_op | source)
XLA Modules:
  0.0 36.1 jit_solution(14665246749258470794)
XLA Ops:
  0.6 0.0 copy-start
  0.6 1.5 %copy-done = f32[30,8,2048]{2,1,0:T(8,128)S(1)} copy-done((f32[30,8,2048]{2,1,0:T(8,128)S(1)}, f32[30,8,2048]{2,1,0:T(8,128)}, u32[]{:S(2)}) %copy-start) | copy-done | bytes 1966104
  2.2 0.0 copy-start.1
  2.2 0.8 %copy-done.1 = s32[3,2048]{1,0:T(4,128)S(1)} copy-done((s32[3,2048]{1,0:T(4,128)S(1)}, s32[3,2048]{1,0:T(4,128)}, u32[]{:S(2)}) %copy-start.1) | copy-done | bytes 24600
  2.9 0.0 copy-start.2
  2.9 0.7 %copy-done.2 = s32[2048]{0:T(1024)S(1)} copy-done((s32[2048]{0:T(1024)S(1)}, s32[2048]{0:T(1024)}, u32[]{:S(2)}) %copy-start.2) | copy-done | bytes 8216
  3.6 0.0 copy-start.3
  3.6 0.7 %copy-done.3 = f32[16]{0:T(128)S(1)} copy-done((f32[16]{0:T(128)S(1)}, f32[16]{0:T(128)}, u32[]{:S(2)}) %copy-start.3) | copy-done | bytes 88
  4.3 29.7 %foldy_step.1 = (f32[8,256]{1,0:T(8,128)S(1)}, f32[8,128]{1,0:T(8,128)S(1)}, f32[8,2048]{1,0:T(8,128)S(1)}) custom-call(f32[16]{0:T(128)S(1)} %copy-done.3, f32[240,2048]{1,0:T(8,128)S(1)} %bitcast.9, s32[3,2048]{1,0:T(4,128)S(1)} %copy-done.1, s32[1,2048]{1,0:T(1,128)S(1)} %bitcast.10), custom_call_target="tpu_custom_call" | custom-call | tf_op jit(solution)/shard_map/foldy_step/pallas_call | solution.py:326
  34.0 0.1 slice_bitcast_fusion.2
  34.0 0.6 %pad_maximum_fusion = f32[2,4,4]{2,1,0:T(4,128)} fusion(f32[1,4,4]{2,1,0:T(4,128)S(1)} %get-tuple-element.13, f32[1,4,4]{2,1,0:T(4,128)S(1)} %get-tuple-element.12), kind=kLoop, calls=%fused_computation.1 | loop fusion | flops 32 | bytes 256 | tf_op jit(solution)/shard_map/stack | solution.py:367
  34.6 0.1 reshape.17
  34.8 0.7 %copy.8 = f32[30,2,4,4]{0,3,2,1:T(4,128)} copy(f32[30,2,4,4]{2,0,3,1:T(8,128)S(1)} %slice_bitcast_fusion) | data formatting | bytes 7680
  35.5 0.6 %copy.10 = f32[8,2048]{1,0:T(8,128)} copy(f32[8,2048]{1,0:T(8,128)S(1)} %get-tuple-element.17) | data formatting | bytes 131072
  (1 shorter events, 0.0 us)
Async XLA Ops:
  0.6 1.5 %copy-start = (f32[30,8,2048]{2,1,0:T(8,128)S(1)}, f32[30,8,2048]{2,1,0:T(8,128)}, u32[]{:S(2)}) copy-start(f32[30,8,2048]{2,1,0:T(8,128)} %param.4) | copy-start | bytes 5898244
  2.2 0.8 %copy-start.1 = (s32[3,2048]{1,0:T(4,128)S(1)}, s32[3,2048]{1,0:T(4,128)}, u32[]{:S(2)}) copy-start(s32[3,2048]{1,0:T(4,128)} %lattice_hbm.1) | copy-start | bytes 73732
  2.9 0.7 %copy-start.2 = (s32[2048]{0:T(1024)S(1)}, s32[2048]{0:T(1024)}, u32[]{:S(2)}) copy-start(s32[2048]{0:T(1024)} %param.6) | copy-start | bytes 24580
  3.6 0.7 %copy-start.3 = (f32[16]{0:T(128)S(1)}, f32[16]{0:T(128)}, u32[]{:S(2)}) copy-start(f32[16]{0:T(128)} %table_hbm.1) | copy-start | bytes 196

commit v3 on v2

--- a/solution.py
+++ b/solution.py
@@ -145,7 +145,6 @@
     ]
     zeros = jnp.zeros((8, T), f32)
     tgt[...] = jnp.concatenate([features(lattice_ref[...], False), zeros], 0).astype(bf16)
-    pl.semaphore_wait(barrier, R - 1 + parts - 1)
 
     def row_copy(ref, sends, recvs, slot, peer):
         return pltpu.make_async_remote_copy(
@@ -163,9 +162,6 @@
             copy = row_copy(ref, sends, recvs, peer, peer)
             copy.wait_recv()
             copy.wait_send()
-
-    row_send(gath, send1, recv1)
-    loads[4].wait()
 
     def scatter(chunk, part, masked=False):
         block = gath[pl.ds(chunk, 1)][0].astype(f32)
@@ -181,32 +177,57 @@
             turned, imag_part, preferred_element_type=f32
         )
 
-    def target_of(k):
-        left = parts - 1 - k
-        to_col = lax.rem(col + left // G, C)
+    def target_of(left):
+        left_col = lax.div(left, G)
+        if C & (C - 1):
+            to_col = lax.rem(col + left_col, C)
+        else:
+            to_col = 0
+            for bit in range(C.bit_length() - 1):
+                size = 1 << bit
+                to_col = to_col + lax.rem(lax.div(col, size) + lax.div(left_col, size), 2) * size
         to_grp = lax.rem(grp + left, G)
         return to_col, to_grp
 
-    def first_part(part, masked):
+    def basis_slice(part):
         at = pl.ds(pl.multiple_of(part * blk, blk), blk)
         b_high, b_low = split(basis[:, at])
         high[:, at] = b_high
         low[:, at] = b_low
+        return b_high, b_low
+
+    def store_first(part, masked):
+        partial[pl.ds(part, 1)] = scatter(row, part, masked)[None]
+
+    store_first(me, True)
+    early = max(parts // 2, 1)
+
+    @pl.loop(1, early)
+    def _(left):
+        to_col, to_grp = target_of(left)
+        store_first(to_col * G + to_grp, False)
+
+    pl.semaphore_wait(barrier, R - 1 + parts - 1)
+    row_send(gath, send1, recv1)
+    loads[4].wait()
+    late = parts - early
+    each = parts // late
+
+    @pl.loop(early, parts)
+    def _(left):
+        to_col, to_grp = target_of(left)
+        store_first(to_col * G + to_grp, False)
+        left_part, right_part = [], []
+        for i in range(each):
+            b_high, b_low = basis_slice((left - early) * each + i)
+            left_part += [b_high, b_low, b_high]
+            right_part += [b_high, b_high, b_low]
         products = lax.dot_general(
-            jnp.concatenate([b_high, b_low, b_high], 1),
-            jnp.concatenate([b_high, b_high, b_low], 1),
-            lanes, preferred_element_type=f32,
+            jnp.concatenate(left_part, 1), jnp.concatenate(right_part, 1), lanes,
+            preferred_element_type=f32,
         )
         for p in range(planes):
             overlap[p] += products[:, p * 128:(p + 1) * 128]
-        partial[pl.ds(part, 1)] = scatter(row, part, masked)[None]
-
-    @pl.loop(0, parts - 1)
-    def _(k):
-        to_col, to_grp = target_of(k)
-        first_part(to_col * G + to_grp, False)
-
-    first_part(me, True)
 
     for a in range(half):
         for p in range(planes):
@@ -226,7 +247,7 @@
 
     @pl.loop(0, parts)
     def _(k):
-        to_col, to_grp = target_of(k)
+        to_col, to_grp = target_of(parts - 1 - k)
         part = to_col * G + to_grp
 
         def more(q, total):
@@ -260,25 +281,40 @@
             device_id_type=MESH,
         )
 
-    for k in range(1, parts):
-        field_copy(me, lax.rem(me + k, parts)).start()
-    for k in range(1, parts):
-        other = lax.rem(me + k, parts)
+    def peer_of(left):
+        to_col, to_grp = target_of(jnp.int32(left))
+        return to_col * G + to_grp
+
+    for left in range(parts - 1, 0, -1):
+        field_copy(me, peer_of(left)).start()
+
+    def stack(x):
+        x_high, x_low = split(x)
+        return jnp.concatenate([x_high.astype(f32), x_low.astype(f32)], 0).astype(bf16)
+
+    def piece(part):
+        at = pl.ds(pl.multiple_of(part * blk, blk), blk)
+        stacked = stack(field[:, at])
+        out = lax.dot_general(
+            jnp.concatenate([stacked, stacked], 1),
+            jnp.concatenate([high[:, at], low[:, at]], 1),
+            lanes, preferred_element_type=f32,
+        )
+        norm = lax.dot_general(stacked, stacked, lanes, preferred_element_type=f32)
+        return out, norm
+
+    out, norm = piece(me)
+    for left in range(1, parts):
+        other = peer_of(left)
         copy = field_copy(other, other)
         copy.wait_recv()
         copy.wait_send()
-
-    def product(x, numbers):
-        x_high, x_low = split(x)
-        stacked = jnp.concatenate([x_high.astype(f32), x_low.astype(f32)], 0).astype(bf16)
-        out = lax.dot_general(stacked, high[...], numbers, preferred_element_type=f32)
-        out = out + lax.dot_general(stacked, low[...], numbers, preferred_element_type=f32)
-        return out[:8] + out[8:]
-
-    scattered = field[...]
-    coef[pl.ds(row, 1), :, :KP] = product(scattered, lanes)[None]
+        more_out, more_norm = piece(other)
+        out, norm = out + more_out, norm + more_norm
+    coef[pl.ds(row, 1), :, :KP] = (out[:ch] + out[ch:])[None]
     coef[pl.ds(row, 1), :, KP:] = jnp.zeros((1, ch, 128), f32)
-    coef[pl.ds(row, 1), :, pl.ds(KP, ch)] = dot(scattered, scattered, lanes)[None]
+    norm = norm[:ch] + norm[ch:]
+    coef[pl.ds(row, 1), :, pl.ds(KP, ch)] = (norm[:, :ch] + norm[:, ch:])[None]
     row_send(coef, send4, recv4)
 
     scale = 1.0 / points
@@ -290,24 +326,32 @@
             at = slice(p * 128, (p + 1) * 128)
             metric[p, pl.ds(a, blocks, stride=ch), :] = rows[:, at]
             metric[p, pl.ds(a + half, blocks, stride=ch), :] = turned[:, at]
+    full = jnp.concatenate([metric[p] for p in range(planes)], 1)
+    full_high, full_low = split(full)
+
+    def apply(x, x_high, x_low):
+        stacked = stack(x)
+        out = jnp.dot(stacked, x_high, preferred_element_type=f32)
+        out = out + jnp.dot(stacked, x_low, preferred_element_type=f32)
+        return out[:ch] + out[ch:]
+
     row_wait(coef, send4, recv4)
     sums = jnp.sum(coef[...], 0) * scale
     mixed = lift(sums[:, :KP])
     self_gram = lift(sums[:, KP:])[:, :ch]
-    full = jnp.concatenate([metric[p] for p in range(planes)], 1)
     once = full[K - ch:K] - mixed
-    twice = once - dot(once, full)
+    twice = once - apply(once, full_high, full_low)
     both = once + twice
     coef_ref[...] = both
     at_row = lax.broadcasted_iota(jnp.int32, both.shape, 0)
     at_lane = lax.broadcasted_iota(jnp.int32, both.shape, 1)
     change = both - jnp.where(at_lane == at_row + (K - ch), 1.0, 0.0)
-    new_ref[...] = -(scattered + product(change, (((1,), (0,)), ((), ()))))
+    new_ref[...] = -(field[...] + apply(change, high[...], low[...]))
     cross = dot(mixed, change, lanes)
     cross_t = dot(change, mixed, lanes)
     gram_ref[...] = jnp.zeros_like(gram_ref)
     gram_ref[:, :ch] = self_gram + cross + cross_t + dot(
-        dot(change, full), change, lanes
+        apply(change, full_high, full_low), change, lanes
     )
 
 
@@ -357,7 +401,7 @@
             dma((R,)), dma((R,)),
         ],
         compiler_params=pltpu.CompilerParams(
-            collective_id=0, has_side_effects=True, vmem_limit_bytes=48 * 1024 * 1024
+            collective_id=0, has_side_effects=True, vmem_limit_bytes=67043328
         ),
         name="foldy_step",
     )(strength_table, krylov_basis.reshape(K, T), lattice, strength_index.reshape(1, T))

time: 36.4 us -> 34.4 us (0.945)
  local copies, waits for them, and re-layouts: 5.18 us -> 3.83 us
  Pallas kernels: 29.7 us -> 29.1 us
    unnamed x10 -> x2, local copies, waits for them, and re-layouts: 5 us -> 2.2 us
    another operation x1, local copies, waits for them, and re-layouts: 0.07 us -> 0.83 us  [local(): block_gram = jnp.stack([gram[:half, :half], gram[:half, half:ch]], 0)]
    reshape x1, local copies, waits for them, and re-layouts: 0.1 us -> 0.79 us  [local(): mixing = coefs[:, :K].reshape(2, half, nb, ch)[..., :half]]
    pallas_call x1, Pallas kernels: 29.7 us -> 29.1 us  [local(): pl.pallas_call(functools.partial(kernel, dims), out_shape=(jax.ShapeDtype...]
where the time goes in v3:
time: 34.4 us; the launch traced here: 34.2 us
  Pallas kernels  29.1 us (85%)
  local copies, waits for them, and re-layouts  3.83 us (11%)
  between operations  0.66 us (2%)
  other arithmetic  0.6 us (2%)
    pallas_call x1, Pallas kernels, local(): pl.pallas_call(functools.partial(kernel, dims), out_shape=(jax.ShapeDtype...  29.1 us
    unnamed x2, local copies, waits for them, and re-layouts  2.2 us
    another operation x1, local copies, waits for them, and re-layouts, local(): block_gram = jnp.stack([gram[:half, :half], gram[:half, half:ch]], 0)  0.83 us
    reshape x1, local copies, waits for them, and re-layouts, local(): mixing = coefs[:, :K].reshape(2, half, nb, ch)[..., :half]  0.79 us

profile of v3, /device:TPU:0, one launch (start us, length us, event | category | flops | bytes accessed | tf_op | source)
XLA Modules:
  0.0 34.2 jit_solution(14800781826117392473)
XLA Ops:
  0.6 29.1 %foldy_step.1 = (f32[8,256]{1,0:T(8,128)}, f32[8,128]{1,0:T(8,128)}, f32[8,2048]{1,0:T(8,128)}) custom-call(f32[16]{0:T(128)} %table_hbm.1, f32[240,2048]{1,0:T(8,128)} %bitcast.9, s32[3,2048]{1,0:T(4,128)} %lattice_hbm.1, s32[1,2048]{1,0:T(1,128)} %bitcast.10), custom_call_target="tpu_custom_call" | custom-call | tf_op jit(solution)/shard_map/foldy_step/pallas_call | solution.py:370
  29.7 0.8 %slice_bitcast_fusion.2 = (f32[1,4,4]{2,1,0:T(4,128)S(1)}, f32[1,4,4]{2,1,0:T(4,128)S(1)}) fusion(f32[8,128]{1,0:T(8,128)} %get-tuple-element.8), kind=kLoop, calls=%fused_computation.3 | loop fusion | bytes 256 | tf_op jit(solution)/shard_map/stack | solution.py:411
  30.5 0.6 %pad_maximum_fusion = f32[2,4,4]{2,1,0:T(4,128)} fusion(f32[1,4,4]{2,1,0:T(4,128)S(1)} %get-tuple-element.13, f32[1,4,4]{2,1,0:T(4,128)S(1)} %get-tuple-element.12), kind=kLoop, calls=%fused_computation.1 | loop fusion | flops 32 | bytes 256 | tf_op jit(solution)/shard_map/stack | solution.py:411
  31.1 0.8 %reshape.17 = f32[2,4,30,8]{3,2,1,0:T(8,128)S(1)} reshape(f32[8,240]{1,0:T(8,128)} %bitcast.11) | data formatting | bytes 15360 | tf_op jit(solution)/shard_map/reshape | solution.py:409
  32.0 0.7 %copy.8 = f32[30,2,4,4]{0,3,2,1:T(4,128)} copy(f32[30,2,4,4]{2,0,3,1:T(8,128)S(1)} %slice_bitcast_fusion) | data formatting | bytes 7680
  32.7 1.5 %copy.10 = f32[8,2048]{1,0:T(8,128)} copy(f32[8,2048]{1,0:T(8,128)} %get-tuple-element.17) | data formatting | bytes 131072
  (1 shorter events, 0.0 us)

commit v4 on v3

--- a/solution.py
+++ b/solution.py
@@ -401,10 +401,10 @@
             dma((R,)), dma((R,)),
         ],
         compiler_params=pltpu.CompilerParams(
-            collective_id=0, has_side_effects=True, vmem_limit_bytes=67043328
+            collective_id=0, has_side_effects=True, vmem_limit_bytes=50331648
         ),
         name="foldy_step",
-    )(strength_table, krylov_basis.reshape(K, T), lattice, strength_index.reshape(1, T))
+    )(*[pltpu.with_memory_space_constraint(v, pltpu.HBM) for v in (strength_table, krylov_basis.reshape(K, T), lattice, strength_index.reshape(1, T))])
     half = ch // 2
     mixing = coefs[:, :K].reshape(2, half, nb, ch)[..., :half]
     hessenberg = mixing.transpose(2, 0, 3, 1)

time: 34.4 us -> 31.4 us (0.913)
  local copies, waits for them, and re-layouts: 3.83 us -> 1.54 us
  Pallas kernels: 29.1 us -> 28.5 us
    unnamed x2, local copies, waits for them, and re-layouts: 2.2 us -> 1.36 us
    another operation x1, local copies, waits for them, and re-layouts: 0.83 us -> 0.07 us  [local(): block_gram = jnp.stack([gram[:half, :half], gram[:half, half:ch]], 0)]
    reshape x1, local copies, waits for them, and re-layouts: 0.79 us -> 0.1 us  [local(): mixing = coefs[:, :K].reshape(2, half, nb, ch)[..., :half]]
    pallas_call x1, Pallas kernels: 29.1 us -> 28.5 us  [local(): pl.pallas_call(functools.partial(kernel, dims), out_shape=(jax.ShapeDtype...]
where the time goes in v4:
time: 31.4 us; the launch traced here: 31.2 us
  Pallas kernels  28.5 us (91%)
  local copies, waits for them, and re-layouts  1.54 us (5%)
  between operations  0.66 us (2%)
  other arithmetic  0.6 us (2%)
    pallas_call x1, Pallas kernels, local(): pl.pallas_call(functools.partial(kernel, dims), out_shape=(jax.ShapeDtype...  28.5 us
    unnamed x2, local copies, waits for them, and re-layouts  1.36 us

profile of v4, /device:TPU:0, one launch (start us, length us, event | category | flops | bytes accessed | tf_op | source)
XLA Modules:
  0.0 31.2 jit_solution(6997632989918281064)
XLA Ops:
  0.6 28.5 %foldy_step.1 = (f32[8,256]{1,0:T(8,128)S(1)}, f32[8,128]{1,0:T(8,128)S(1)}, f32[8,2048]{1,0:T(8,128)S(1)}) custom-call(f32[16]{0:T(128)} %table_hbm.1, f32[240,2048]{1,0:T(8,128)} %bitcast.10, s32[3,2048]{1,0:T(4,128)} %lattice_hbm.1, s32[1,2048]{1,0:T(1,128)} %bitcast.11), custom_call_target="tpu_custom_call" | custom-call | tf_op jit(solution)/shard_map/foldy_step/pallas_call | solution.py:370
  29.1 0.1 slice_bitcast_fusion.2
  29.2 0.6 %pad_maximum_fusion = f32[2,4,4]{2,1,0:T(4,128)} fusion(f32[1,4,4]{2,1,0:T(4,128)S(1)} %get-tuple-element.13, f32[1,4,4]{2,1,0:T(4,128)S(1)} %get-tuple-element.12), kind=kLoop, calls=%fused_computation.1 | loop fusion | flops 32 | bytes 256 | tf_op jit(solution)/shard_map/stack | solution.py:411
  29.8 0.1 reshape.17
  29.9 0.7 %copy.8 = f32[30,2,4,4]{0,3,2,1:T(4,128)} copy(f32[30,2,4,4]{2,0,3,1:T(8,128)S(1)} %slice_bitcast_fusion) | data formatting | bytes 7680
  30.6 0.6 %copy.10 = f32[8,2048]{1,0:T(8,128)} copy(f32[8,2048]{1,0:T(8,128)S(1)} %get-tuple-element.17) | data formatting | bytes 131072
  (1 shorter events, 0.0 us)

commit v5 on v4

--- a/solution.py
+++ b/solution.py
@@ -220,8 +220,8 @@
         left_part, right_part = [], []
         for i in range(each):
             b_high, b_low = basis_slice((left - early) * each + i)
-            left_part += [b_high, b_low, b_high]
-            right_part += [b_high, b_high, b_low]
+            left_part += [b_high, b_high]
+            right_part += [b_high * bf16(0.5), b_low]
         products = lax.dot_general(
             jnp.concatenate(left_part, 1), jnp.concatenate(right_part, 1), lanes,
             preferred_element_type=f32,
@@ -229,6 +229,10 @@
         for p in range(planes):
             overlap[p] += products[:, p * 128:(p + 1) * 128]
 
+    summed = jnp.concatenate([overlap[p] for p in range(planes)], 1)
+    summed = summed + summed.T
+    for p in range(planes):
+        overlap[p] = summed[:, p * 128:(p + 1) * 128]
     for a in range(half):
         for p in range(planes):
             upper = overlap[p, pl.ds(a, blocks, stride=ch), :]

time: 31.4 us -> 31.3 us (level)
  no operation moved by 1% of the time
where the time goes in v5:
time: 31.3 us; the launch traced here: 31.2 us
  Pallas kernels  28.4 us (91%)
  local copies, waits for them, and re-layouts  1.54 us (5%)
  between operations  0.66 us (2%)
  other arithmetic  0.6 us (2%)
    pallas_call x1, Pallas kernels, local(): pl.pallas_call(functools.partial(kernel, dims), out_shape=(jax.ShapeDtype...  28.4 us
    unnamed x2, local copies, waits for them, and re-layouts  1.36 us

profile of v5, /device:TPU:0, one launch (start us, length us, event | category | flops | bytes accessed | tf_op | source)
XLA Modules:
  0.0 31.2 jit_solution(9904457637429938225)
XLA Ops:
  0.6 28.4 %foldy_step.1 = (f32[8,256]{1,0:T(8,128)S(1)}, f32[8,128]{1,0:T(8,128)S(1)}, f32[8,2048]{1,0:T(8,128)S(1)}) custom-call(f32[16]{0:T(128)} %table_hbm.1, f32[240,2048]{1,0:T(8,128)} %bitcast.10, s32[3,2048]{1,0:T(4,128)} %lattice_hbm.1, s32[1,2048]{1,0:T(1,128)} %bitcast.11), custom_call_target="tpu_custom_call" | custom-call | tf_op jit(solution)/shard_map/foldy_step/pallas_call | solution.py:374
  29.0 0.1 slice_bitcast_fusion.2
  29.1 0.6 %pad_maximum_fusion = f32[2,4,4]{2,1,0:T(4,128)} fusion(f32[1,4,4]{2,1,0:T(4,128)S(1)} %get-tuple-element.13, f32[1,4,4]{2,1,0:T(4,128)S(1)} %get-tuple-element.12), kind=kLoop, calls=%fused_computation.1 | loop fusion | flops 32 | bytes 256 | tf_op jit(solution)/shard_map/stack | solution.py:415
  29.7 0.1 reshape.17
  29.8 0.7 %copy.8 = f32[30,2,4,4]{0,3,2,1:T(4,128)} copy(f32[30,2,4,4]{2,0,3,1:T(8,128)S(1)} %slice_bitcast_fusion) | data formatting | bytes 7680
  30.6 0.6 %copy.10 = f32[8,2048]{1,0:T(8,128)} copy(f32[8,2048]{1,0:T(8,128)S(1)} %get-tuple-element.17) | data formatting | bytes 131072
  (1 shorter events, 0.0 us)
